TPU v7x, 8 devices: a whole 2x2x1 slice. The times are simulated.
8 devices in a mesh: data: 1 (over z), fsdp: 2 (over y), tp: 4 (over x, core).
Axes of the slice: x: 2, y: 2, z: 1, core: 2. Of those that a mesh axis runs over, the one named last changes fastest.
Arguments:
- hidden: bfloat16 [16384, 5120], P(('data', 'fsdp', 'tp'))
- ln_scale: float32 [5120], replicated
- w_in: bfloat16 [5120, 13824], P('fsdp', 'tp')
- w_out: bfloat16 [13824, 5120], P(('tp', 'fsdp'))
Outputs:
- output: bfloat16 [16384, 5120], P(('data', 'fsdp', 'tp'))
All inputs are finite; a program needn't handle non-finite values.
Results may differ from a plain program's by a relative error of at most 0.001.
Values are sent between devices in bfloat16 or wider.
A program may use at most 1 GiB of HBM per device.

v0:
```python
import jax
import jax.numpy as jnp
from jax import lax
from jax.sharding import PartitionSpec as P, NamedSharding

LN_EPS = 1e-6


def layer_norm(row_block, ln_scale):
    block_f32 = row_block.astype(jnp.float32)
    centered = block_f32 - jnp.mean(block_f32, axis=-1, keepdims=True)
    var_row = jnp.mean(centered * centered, axis=-1, keepdims=True)
    return (centered * lax.rsqrt(var_row + LN_EPS) * ln_scale).astype(jnp.bfloat16)


def solution(mesh):
    def local_mlp(hidden, ln_scale, w_in, w_out):
        normed = layer_norm(hidden, ln_scale)
        w_in_tp = lax.all_gather(w_in, "fsdp", axis=0, tiled=True)
        w_out_tp = lax.all_gather(w_out, "fsdp", axis=0, tiled=True)
        group_normed = lax.all_gather(normed, "tp", axis=0, tiled=True)
        pre_act = jnp.dot(group_normed, w_in_tp, preferred_element_type=jnp.float32)
        act_out = jax.nn.gelu(pre_act, approximate=True).astype(jnp.bfloat16)
        part_sum = jnp.dot(act_out, w_out_tp, preferred_element_type=jnp.float32)
        mlp_out = lax.psum_scatter(part_sum, "tp", scatter_dimension=0, tiled=True)
        return (hidden.astype(jnp.float32) + mlp_out).astype(jnp.bfloat16)

    return jax.shard_map(
        local_mlp,
        mesh=mesh,
        in_specs=(P(("data", "fsdp", "tp"), None), P(None), P("fsdp", "tp"), P(("tp", "fsdp"), None)),
        out_specs=P(("data", "fsdp", "tp"), None),
        check_vma=False,
    )
```

profile of v0, /device:TPU:0, one launch (start us, length us, event | category | flops | bytes accessed | tf_op | source)
XLA Modules:
  0.0 2818.2 jit_solution(15007109520143402959)
XLA Ops:
  6.5 0.0 all-gather.6.cloned.1.call-start
  6.5 0.7 all-gather.6.cloned.1.call-update
  7.3 0.0 all-gather.4.cloned.1.call-start
  7.3 0.0 slice-start
  7.3 0.0 slice-start.1
  7.3 0.0 slice-start.2
  7.3 10.9 convert_reduce_fusion
  18.2 0.0 slice-start.3
  18.2 0.0 slice-start.4
  18.3 11.2 fusion.16
  29.4 0.0 copy-done
  29.5 12.0 fusion.18
  41.5 0.0 all-gather.4.cloned.1.call-update
  41.5 0.0 all-gather.8.cloned.1.call-start
  41.6 0.7 all-gather.8.cloned.1.call-update
  42.3 0.0 reduce-scatter.4.cloned.1.call-start
  42.3 377.3 %all-gather.6.cloned.1.call-done = bf16[5120,3456]{1,0:T(8,128)(2,1)} async-done(((bf16[2560,3456]{1,0:T(8,128)(2,1)}), bf16[5120,3456]{1,0:T(8,128)(2,1)}) %all-gather.6.cloned.1.call-update) | async-done | bytes 35389456 | tf_op jit(solution)/shard_map/all_gather | solution.py:19
  419.6 486.4 %all-gather.4.cloned.1.call-done = bf16[8192,5120]{1,0:T(8,128)(2,1)} async-done(((bf16[2048,5120]{1,0:T(8,128)(2,1)}), bf16[8192,5120]{1,0:T(8,128)(2,1)}) %all-gather.4.cloned.1.call-update) | async-done | bytes 83886096 | tf_op jit(solution)/shard_map/all_gather | solution.py:21
  906.0 321.3 %fusion.24 = f32[8192,3456]{1,0:T(8,128)} fusion(bf16[8192,5120]{1,0:T(8,128)(2,1)} %all-gather.4.cloned.1.call-done, bf16[5120,3456]{1,0:T(8,128)(2,1)} %all-gather.6.cloned.1.call-done), kind=kOutput, calls=%fused_computation.29 | convolution fusion | flops 289910292480 | bytes 232521728 | tf_op jit(solution)/shard_map/dot_general | solution.py:22
  1227.4 88.2 %all-gather.8.cloned.1.call-done = bf16[3456,5120]{1,0:T(8,128)(2,1)} async-done(((bf16[1728,5120]{1,0:T(8,128)(2,1)}), bf16[3456,5120]{1,0:T(8,128)(2,1)}) %all-gather.8.cloned.1.call-update) | async-done | bytes 35389456 | tf_op jit(solution)/shard_map/all_gather | solution.py:20
  1315.5 399.0 %fusion.8 = f32[8192,5120]{1,0:T(8,128)} fusion(bf16[3456,5120]{1,0:T(8,128)(2,1)} %all-gather.8.cloned.1.call-done, f32[8192,3456]{1,0:T(8,128)} %fusion.24), kind=kOutput, calls=%fused_computation.12 | convolution fusion | flops 290165096448 | bytes 316407808 | tf_op jit(solution)/shard_map/dot_general | solution.py:24
  1714.5 0.0 reduce-scatter.4.cloned.1.call-update
  1714.6 1069.6 %reduce-scatter.4.cloned.1.call-done = f32[2048,5120]{1,0:T(8,128)} async-done(((f32[8192,5120]{1,0:T(8,128)}), f32[2048,5120]{1,0:T(8,128)}) %reduce-scatter.4.cloned.1.call-update) | async-done | bytes 41943056
  2784.2 27.5 fusion.19
  (9 shorter events, 0.0 us)
Async XLA Ops:
  6.5 22.9 copy-start
  6.5 413.1 %all-gather.6.cloned.1.call-start = ((), (), s32[]{:S(2)}) async-start(), calls=%async_computation.2 | async-start | bytes 53084160 | tf_op jit(solution)/shard_map/all_gather | solution.py:19
  7.3 898.8 %all-gather.4.cloned.1.call-start = ((), (), s32[]{:S(2)}) async-start(), calls=%async_computation.1 | async-start | bytes 104857600 | tf_op jit(solution)/shard_map/all_gather | solution.py:21
  7.3 22.2 slice-start
  7.3 22.1 slice-start.1
  7.3 22.1 slice-start.2
  18.2 11.3 slice-start.3
  18.2 11.3 slice-start.4
  41.5 1274.0 %all-gather.8.cloned.1.call-start = ((), (), s32[]{:S(2)}) async-start(), calls=%async_computation.3 | async-start | bytes 53084160 | tf_op jit(solution)/shard_map/all_gather | solution.py:20
  42.3 2741.9 %reduce-scatter.4.cloned.1.call-start = ((), (), s32[]{:S(2)}) async-start(), calls=%async_computation.4 | async-start | bytes 209715200
Sparse Core Ops, SparseCore 0:
  8.9 410.7 all-gather.5
  421.2 484.8 all-gather.3
  907.6 407.9 all-gather.7
  1714.7 1069.4 reduce-scatter.3
where the time goes:
time: 2820 us
  waiting for transfers between devices  2020 us (72%)
  matrix products  720 us (26%)
  other arithmetic  61.6 us (2%)
    unnamed x5, waiting for transfers between devices  1070 us
    all_gather x1, waiting for transfers between devices, local_mlp(): group_normed = lax.all_gather(normed, 'tp', axis=0, tiled=True)  486 us
    dot_general x1, matrix products, local_mlp(): part_sum = jnp.dot(act_out, w_out_tp, preferred_element_type=jnp.float32)  399 us
    all_gather x1, waiting for transfers between devices, local_mlp(): w_in_tp = lax.all_gather(w_in, 'fsdp', axis=0, tiled=True)  377 us
    dot_general x1, matrix products, local_mlp(): pre_act = jnp.dot(group_normed, w_in_tp, preferred_element_type=jnp.float32)  321 us
    all_gather x1, waiting for transfers between devices, local_mlp(): w_out_tp = lax.all_gather(w_out, 'fsdp', axis=0, tiled=True)  88.2 us
  transfers between devices with their start and end apart: 4, of which 4 were waited for; matrix products, arithmetic and copies ran while one was open for 13% of the time, Pallas kernels for 0%

commit v1 on v0

v1 whole, which is shorter than its diff:
```python
import jax
import jax.numpy as jnp
from jax import lax
from jax.experimental import pallas as pl
from jax.experimental.pallas import tpu as pltpu
from jax.sharding import PartitionSpec as P

LN_EPS = 1e-6
MESH = pl.DeviceIdType.MESH

ROWS, DIM, FFN = 2048, 5120, 13824
K_PIECE, F_BLOCK = 2560, 3456
F_PIECE = 1728
CA, NA = 128, 27
CB, NB = 256, 20
S = NA + NB
LEAD = 2
TM = 256
MT = ROWS // TM
NPAIR = 8


def kernel(hid, gain, w_in, w_out, out, g1, g2, hbm_h,
           r_x, r_y, r_dx, r_dy, r_c, s_sem, ld_sem, t_sem, o_sem):
    f = lax.axis_index("fsdp")
    t = lax.axis_index("tp")
    x, k = t // 2, t % 2
    xn = {"tp": 2 * (1 - x) + k}
    yn = {"fsdp": 1 - f}
    cn = {"tp": 2 * x + 1 - k}
    me = (f, x, k)
    px, py, pd = (f, 1 - x, k), (1 - f, x, k), (1 - f, 1 - x, k)

    def piece_a(i, who, half=None):
        wf, wx, wk = who
        n = K_PIECE if half is None else K_PIECE // 2
        r0 = wf * K_PIECE + (0 if half is None else half * n)
        return g1.at[i, pl.ds(pl.multiple_of(r0, 128), n),
                     pl.ds(pl.multiple_of((2 * wx + wk) * CA, 128), CA)]

    def piece_b(j, who, half=None):
        wf, wx, wk = who
        n = F_PIECE if half is None else F_PIECE // 2
        r0 = (2 * wx + wk) * F_BLOCK + wf * F_PIECE + (0 if half is None else half * n)
        return g2.at[pl.ds(pl.multiple_of(r0, 32), n),
                     pl.ds(pl.multiple_of(j * CB, 128), CB)]

    def own_a(i):
        return w_in.at[:, pl.ds(pl.multiple_of(i * CA, 128), CA)]

    def own_b(j):
        return w_out.at[:, pl.ds(pl.multiple_of(j * CB, 128), CB)]

    def rc(src, dst, kind, ph, recv, dev):
        return pltpu.make_async_remote_copy(
            src, dst, s_sem.at[ph, kind], recv, device_id=dev, device_id_type=MESH)

    phases = ((0, piece_a, own_a, 0, NA), (1, piece_b, own_b, NA, S))

    def each_phase(i, body):
        if isinstance(i, int):
            for ph, piece, own, lo, hi in phases:
                if lo <= i < hi:
                    body(ph, piece, own, i - lo)
            return
        for ph, piece, own, lo, hi in phases:
            pl.when(jnp.logical_and(i >= lo, i < hi))(
                lambda ph=ph, piece=piece, own=own, lo=lo: body(ph, piece, own, i - lo))

    def send_own(i):
        def body(ph, piece, own, n):
            rc(own(n), piece(n, me), 0, ph, r_x.at[i], xn).start()
            rc(own(n), piece(n, me), 1, ph, r_y.at[i], yn).start()
            rc(own(n), piece(n, me), 2, ph, r_c.at[i], cn).start()
        each_phase(i, body)

    def comm_point(i):
        def body(ph, piece, own, n):
            rc(own(n), piece(n, px), 0, ph, r_x.at[i], xn).wait_recv()
            rc(piece(n, px, 0), piece(n, px, 0), 3, ph, r_dy.at[i], yn).start()
            rc(own(n), piece(n, py), 1, ph, r_y.at[i], yn).wait_recv()
            rc(piece(n, py, 1), piece(n, py, 1), 4, ph, r_dx.at[i], xn).start()
            rc(piece(n, px), piece(n, px), 5, ph, r_c.at[i], cn).start()
            rc(piece(n, py), piece(n, py), 6, ph, r_c.at[i], cn).start()
        each_phase(i, body)
        send_own(i + LEAD)

    def d_point(i):
        def body(ph, piece, own, n):
            rc(piece(n, pd, 0), piece(n, pd, 0), 3, ph, r_dy.at[i], yn).wait_recv()
            rc(piece(n, pd, 0), piece(n, pd, 0), 7, ph, r_c.at[i], cn).start()
            rc(piece(n, pd, 1), piece(n, pd, 1), 4, ph, r_dx.at[i], xn).wait_recv()
            rc(piece(n, pd, 1), piece(n, pd, 1), 8, ph, r_c.at[i], cn).start()
        each_phase(i, body)

    def c_wait(i):
        def body(ph, piece, own, n):
            whole = (g1.at[n, :, pl.ds(0, 2 * CA)] if ph == 0
                     else g2.at[pl.ds(0, 4 * F_PIECE), pl.ds(0, CB)])
            pltpu.make_async_copy(whole, whole, r_c.at[i]).wait()
        each_phase(i, body)

    others = [(a, b, c) for a in (0, 1) for b in (0, 1) for c in (0, 1)][1:]

    def who(d):
        a, b, c = d
        return (1 - f if a else f, 1 - x if b else x, 1 - k if c else k)

    barrier = pltpu.get_barrier_semaphore()
    for nb in (xn, yn, cn):
        pl.semaphore_signal(barrier, inc=1, device_id=nb, device_id_type=MESH)
    pl.semaphore_wait(barrier, 3)
    for i in range(LEAD):
        send_own(i)

    def phase_a(u, w_buf, stage, h_stage, gain_v):
        pltpu.make_async_copy(gain, gain_v, t_sem.at[0]).start()

        def load_rows(m):
            return pltpu.make_async_copy(
                hid.at[pl.ds(m * TM, TM)], stage.at[m % 2], o_sem.at[m % 2, 0])

        load_rows(0).start()
        pltpu.make_async_copy(gain, gain_v, t_sem.at[0]).wait()

        @pl.loop(0, MT)
        def _(m):
            pl.when(m + 1 < MT)(lambda: load_rows(m + 1).start())
            load_rows(m).wait()

            @pl.loop(0, TM // 32)
            def _(r):
                rows = pl.ds(pl.multiple_of(r * 32, 32), 32)
                v = stage[m % 2, rows, :].astype(jnp.float32)
                cen = v - jnp.mean(v, axis=-1, keepdims=True)
                var = jnp.mean(cen * cen, axis=-1, keepdims=True)
                res = cen * lax.rsqrt(var + LN_EPS) * gain_v[...]
                u[pl.ds(pl.multiple_of(m * TM + r * 32, 32), 32), :] = res.astype(jnp.bfloat16)

        def load_w(a):
            slot = a % 2
            for d in others:
                wf, wx, wk = who(d)
                pltpu.make_async_copy(
                    piece_a(a, (wf, wx, wk)),
                    w_buf.at[slot, pl.ds(pl.multiple_of(wf * K_PIECE, 128), K_PIECE),
                             pl.ds(pl.multiple_of((2 * wx + wk) * CA, 128), CA)],
                    ld_sem.at[slot]).start()
            pltpu.make_async_copy(
                own_a(a),
                w_buf.at[slot, pl.ds(pl.multiple_of(f * K_PIECE, 128), K_PIECE),
                         pl.ds(pl.multiple_of(t * CA, 128), CA)],
                ld_sem.at[slot]).start()

        def wait_w(a):
            pltpu.make_async_copy(g1.at[0], w_buf.at[a % 2], ld_sem.at[a % 2]).wait()

        def h_copies(a, m):
            return [pltpu.make_async_copy(
                h_stage.at[m % 2, :, pl.ds(q * CA, CA)],
                hbm_h.at[pl.ds(m * TM, TM), pl.ds(pl.multiple_of(q * F_BLOCK + a * CA, 128), CA)],
                o_sem.at[m % 2, q]) for q in range(4)]

        comm_point(0)

        @pl.loop(0, NA + 1)
        def _(i):
            comm_point(i + 1)
            pl.when(i < NA)(lambda: d_point(i))
            a = i - 1

            @pl.when(i == 0)
            def _():
                c_wait(i)
                load_w(i)

            @pl.when(i > 0)
            def _():
                wait_w(a)

                @pl.loop(0, MT)
                def _(m):
                    @pl.when(jnp.logical_and(m == 2, i < NA))
                    def _():
                        c_wait(i)
                        load_w(i)

                    pre = jnp.dot(u[pl.ds(pl.multiple_of(m * TM, TM), TM), :], w_buf[a % 2],
                                  preferred_element_type=jnp.float32)
                    cdf = 0.5 * (1.0 + jnp.tanh(0.7978845608028654 * (pre + 0.044715 * (pre * pre * pre))))
                    act = (pre * cdf).astype(jnp.bfloat16)

                    @pl.when(jnp.logical_or(a > 0, m >= 2))
                    def _():
                        for c in h_copies(a, m):
                            c.wait()

                    h_stage[m % 2] = act
                    for c in h_copies(a, m):
                        c.start()

        for m in (0, 1):
            for c in h_copies(NA - 1, m):
                c.wait()

    pl.run_scoped(
        phase_a,
        pltpu.VMEM((ROWS, DIM), jnp.bfloat16),
        pltpu.VMEM((2, DIM, 4 * CA), jnp.bfloat16),
        pltpu.VMEM((2, TM, DIM), jnp.bfloat16),
        pltpu.VMEM((2, TM, 4 * CA), jnp.bfloat16),
        pltpu.VMEM((1, DIM), jnp.float32),
    )

    def phase_b(w_buf, h_buf, x_buf, y_buf):
        def load_w(j):
            slot = j % 4
            for d in others:
                wf, wx, wk = who(d)
                r0 = (2 * wx + wk) * F_BLOCK + wf * F_PIECE
                pltpu.make_async_copy(
                    piece_b(j, (wf, wx, wk)),
                    w_buf.at[slot, pl.ds(pl.multiple_of(r0, 32), F_PIECE), :],
                    ld_sem.at[slot]).start()
            r0 = t * F_BLOCK + f * F_PIECE
            pltpu.make_async_copy(
                own_b(j), w_buf.at[slot, pl.ds(pl.multiple_of(r0, 32), F_PIECE), :],
                ld_sem.at[slot]).start()

        def wait_w(j):
            pltpu.make_async_copy(
                g2.at[:, pl.ds(0, CB)], w_buf.at[j % 4], ld_sem.at[j % 4]).wait()

        def load_h(m, slot):
            return pltpu.make_async_copy(
                hbm_h.at[pl.ds(pl.multiple_of(m * TM, TM), TM)], h_buf.at[slot], t_sem.at[slot])

        def load_x(m, j, n, slot):
            return pltpu.make_async_copy(
                hid.at[pl.ds(pl.multiple_of(m * TM, TM), TM),
                       pl.ds(pl.multiple_of(j * CB, 128), n * CB)],
                x_buf.at[slot, :, pl.ds(0, n * CB)], t_sem.at[2 + slot])

        def store_y(m, j, n, slot):
            return pltpu.make_async_copy(
                y_buf.at[slot, :, pl.ds(0, n * CB)],
                out.at[pl.ds(pl.multiple_of(m * TM, TM), TM),
                       pl.ds(pl.multiple_of(j * CB, 128), n * CB)],
                o_sem.at[slot, 0])

        def compute(j, n, hooks):
            for q in range(n):
                wait_w(j + q)
            load_h(0, 0).start()
            load_x(0, j, n, 0).start()

            @pl.loop(0, MT)
            def _(m):
                slot = m % 2

                @pl.when(m + 1 < MT)
                def _():
                    load_h(m + 1, 1 - slot).start()
                    load_x(m + 1, j, n, 1 - slot).start()

                for at, hook in hooks.items():
                    pl.when(m == at)(hook)
                load_h(m, slot).wait()
                load_x(m, j, n, slot).wait()

                @pl.when(m >= 2)
                def _():
                    store_y(m, j, n, slot).wait()

                for q in range(n):
                    cols = slice(q * CB, (q + 1) * CB)
                    acc = jnp.dot(h_buf[slot], w_buf[(j + q) % 4],
                                  preferred_element_type=jnp.float32)
                    y_buf[slot, :, cols] = (
                        x_buf[slot, :, cols].astype(jnp.float32) + acc).astype(jnp.bfloat16)
                store_y(m, j, n, slot).start()

            for m in (MT - 2, MT - 1):
                store_y(m, j, n, m % 2).wait()

        d_point(NA)
        comm_point(NA + 2)
        d_point(NA + 1)
        for n in (0, 1):
            c_wait(NA + n)
            load_w(n)

        @pl.loop(1, NPAIR + 1)
        def _(p):
            j = 2 * p
            comm_point(NA + j + 1)
            d_point(NA + j)

            def mid():
                comm_point(NA + j + 2)
                d_point(NA + j + 1)

            def load():
                for q in (0, 1):
                    c_wait(NA + j + q)
                    load_w(j + q)

            compute(j - 2, 2, {3: mid, 5: load})

        j = 2 * NPAIR

        def next_comm():
            comm_point(NA + j + 3)
            d_point(NA + j + 2)

        def next_load():
            c_wait(NA + j + 2)
            load_w(j + 2)

        def last_d():
            d_point(NA + j + 3)

        def last_load():
            c_wait(NA + j + 3)
            load_w(j + 3)

        compute(j, 1, {})
        compute(j + 1, 1, {0: next_comm, 2: next_load})
        compute(j + 2, 1, {2: last_d, 3: last_load})
        compute(j + 3, 1, {})

    pl.run_scoped(
        phase_b,
        pltpu.VMEM((4, FFN, CB), jnp.bfloat16),
        pltpu.VMEM((2, TM, FFN), jnp.bfloat16),
        pltpu.VMEM((2, TM, 2 * CB), jnp.bfloat16),
        pltpu.VMEM((2, TM, 2 * CB), jnp.bfloat16),
    )

    for kind in range(9):
        rows_a = K_PIECE if kind in (0, 1, 2, 5, 6) else K_PIECE // 2
        pltpu.make_async_copy(w_in.at[pl.ds(0, rows_a)], w_in.at[pl.ds(0, rows_a)],
                              s_sem.at[0, kind]).wait()
        rows_b = F_PIECE if kind in (0, 1, 2, 5, 6) else F_PIECE // 2
        pltpu.make_async_copy(w_out.at[pl.ds(0, rows_b)], w_out.at[pl.ds(0, rows_b)],
                              s_sem.at[1, kind]).wait()


def solution(mesh):
    def local_mlp(hidden, ln_scale, w_in, w_out):
        bf16 = jnp.bfloat16
        y, _, _, _ = pl.pallas_call(
            kernel,
            out_shape=[
                jax.ShapeDtypeStruct((ROWS, DIM), bf16),
                jax.ShapeDtypeStruct((NA, DIM, 4 * CA), bf16),
                jax.ShapeDtypeStruct((FFN, DIM), bf16),
                jax.ShapeDtypeStruct((ROWS, FFN), bf16),
            ],
            in_specs=[pl.BlockSpec(memory_space=pl.ANY)] * 4,
            out_specs=[pl.BlockSpec(memory_space=pl.ANY)] * 4,
            scratch_shapes=[
                pltpu.SemaphoreType.DMA((S,)),
                pltpu.SemaphoreType.DMA((S,)),
                pltpu.SemaphoreType.DMA((S,)),
                pltpu.SemaphoreType.DMA((S,)),
                pltpu.SemaphoreType.DMA((S,)),
                pltpu.SemaphoreType.DMA((2, 9)),
                pltpu.SemaphoreType.DMA((4,)),
                pltpu.SemaphoreType.DMA((4,)),
                pltpu.SemaphoreType.DMA((2, 4)),
            ],
            compiler_params=pltpu.CompilerParams(
                collective_id=0, has_side_effects=True, vmem_limit_bytes=60 * 2**20),
            name="mlp",
        )(hidden, ln_scale.reshape(1, DIM), w_in, w_out)
        return y

    return jax.shard_map(
        local_mlp,
        mesh=mesh,
        in_specs=(P(("data", "fsdp", "tp"), None), P(None), P("fsdp", "tp"), P(("tp", "fsdp"), None)),
        out_specs=P(("data", "fsdp", "tp"), None),
        check_vma=False,
    )
```

time: 2820 us -> 1250 us (0.44)
  waiting for transfers between devices: 2020 us -> 0 us
  Pallas kernels: 0 us -> 1230 us
  matrix products: 720 us -> 0 us
  other arithmetic: 61.6 us -> 0 us
    pallas_call x0 -> x1, Pallas kernels: none -> 1230 us  [local_mlp(): pl.pallas_call(kernel, out_shape=[jax.ShapeDtypeStruct((ROWS, DIM), bf16)...]
    unnamed x5 -> x0, waiting for transfers between devices: 1070 us -> none
    all_gather x3 -> x0, waiting for transfers between devices: 952 us -> none  [the longest x1 486 us: local_mlp(): group_normed = lax.all_gather(normed, 'tp', axis=0, tiled=True)]
    dot_general x2 -> x0, matrix products: 720 us -> none  [the longest x1 399 us: local_mlp(): part_sum = jnp.dot(act_out, w_out_tp, preferred_element_type=jnp.float32)]
    convert_element_type x2 -> x0, other arithmetic: 39.5 us -> none  [the longest x1 27.5 us: local_mlp(): return (hidden.astype(jnp.float32) + mlp_out).astype(jnp.bfloat16)]
  transfers between devices with their start and end apart: 4 -> 0, of which waited for: 4 -> 0; matrix products, arithmetic and copies ran while one was open for 13% -> 0% of each run, Pallas kernels for 0% -> 0%
where the time goes in v1:
time: 1250 us
  Pallas kernels  1230 us (98%)
  local copies, waits for them, and re-layouts  17.3 us (1%)
    pallas_call x1, Pallas kernels, local_mlp(): pl.pallas_call(kernel, out_shape=[jax.ShapeDtypeStruct((ROWS, DIM), bf16)...  1230 us

profile of v1, /device:TPU:0, one launch (start us, length us, event | category | flops | bytes accessed | tf_op | source)
XLA Modules:
  0.0 1245.4 jit_solution(10379242779641089788)
XLA Ops:
  0.0 1228.1 %mlp.1 = (bf16[2048,5120]{1,0:T(8,128)(2,1)}, bf16[27,5120,512]{2,1,0:T(8,128)(2,1)}, bf16[13824,5120]{1,0:T(8,128)(2,1)}, bf16[2048,13824]{1,0:T(8,128)(2,1)}) custom-call(bf16[2048,5120]{1,0:T(8,128)(2,1)} %hid.1, f32[1,5120]{1,0:T(1,128)} %bitcast.1, bf16[2560,3456]{1,0:T(8,128)(2,1)} %w_in.1, bf16[1728,5120]{1,0:T(8,128)(2,1)} %w_out.1), custom_call_target="tpu_custom_call" | custom-call | tf_op jit(solution)/shard_map/mlp/pallas_call | solution.py:352
  1228.1 17.3 %copy.6 = bf16[2048,5120]{1,0:T(8,128)(2,1)} copy(bf16[2048,5120]{1,0:T(8,128)(2,1)} %get-tuple-element.6) | data formatting | bytes 41943040

commit v2 on v1

--- a/solution.py
+++ b/solution.py
@@ -17,11 +17,12 @@
 LEAD = 2
 TM = 256
 MT = ROWS // TM
-NPAIR = 8
+WS = 3
+RES = 1
 
 
 def kernel(hid, gain, w_in, w_out, out, g1, g2, hbm_h,
-           r_x, r_y, r_dx, r_dy, r_c, s_sem, ld_sem, t_sem, o_sem):
+           r_x, r_y, r_dx, r_dy, r_c, r_cd, s_sem, ld_sem, ld2_sem, t_sem, x_sem, o_sem):
     f = lax.axis_index("fsdp")
     t = lax.axis_index("tp")
     x, k = t // 2, t % 2
@@ -88,16 +89,23 @@
     def d_point(i):
         def body(ph, piece, own, n):
             rc(piece(n, pd, 0), piece(n, pd, 0), 3, ph, r_dy.at[i], yn).wait_recv()
-            rc(piece(n, pd, 0), piece(n, pd, 0), 7, ph, r_c.at[i], cn).start()
+            rc(piece(n, pd, 0), piece(n, pd, 0), 7, ph, r_cd.at[i], cn).start()
             rc(piece(n, pd, 1), piece(n, pd, 1), 4, ph, r_dx.at[i], xn).wait_recv()
-            rc(piece(n, pd, 1), piece(n, pd, 1), 8, ph, r_c.at[i], cn).start()
+            rc(piece(n, pd, 1), piece(n, pd, 1), 8, ph, r_cd.at[i], cn).start()
         each_phase(i, body)
 
     def c_wait(i):
         def body(ph, piece, own, n):
-            whole = (g1.at[n, :, pl.ds(0, 2 * CA)] if ph == 0
-                     else g2.at[pl.ds(0, 4 * F_PIECE), pl.ds(0, CB)])
+            whole = (g1.at[n, pl.ds(0, 3 * K_PIECE // 2), pl.ds(0, 2 * CA)] if ph == 0
+                     else g2.at[pl.ds(0, 3 * F_PIECE), pl.ds(0, CB)])
             pltpu.make_async_copy(whole, whole, r_c.at[i]).wait()
+        each_phase(i, body)
+
+    def cd_wait(i):
+        def body(ph, piece, own, n):
+            whole = (g1.at[n, pl.ds(0, K_PIECE // 2), pl.ds(0, 2 * CA)] if ph == 0
+                     else g2.at[pl.ds(0, F_PIECE), pl.ds(0, CB)])
+            pltpu.make_async_copy(whole, whole, r_cd.at[i]).wait()
         each_phase(i, body)
 
     others = [(a, b, c) for a in (0, 1) for b in (0, 1) for c in (0, 1)][1:]
@@ -114,14 +122,14 @@
         send_own(i)
 
     def phase_a(u, w_buf, stage, h_stage, gain_v):
-        pltpu.make_async_copy(gain, gain_v, t_sem.at[0]).start()
+        pltpu.make_async_copy(gain, gain_v, x_sem.at[0]).start()
 
         def load_rows(m):
             return pltpu.make_async_copy(
                 hid.at[pl.ds(m * TM, TM)], stage.at[m % 2], o_sem.at[m % 2, 0])
 
         load_rows(0).start()
-        pltpu.make_async_copy(gain, gain_v, t_sem.at[0]).wait()
+        pltpu.make_async_copy(gain, gain_v, x_sem.at[0]).wait()
 
         @pl.loop(0, MT)
         def _(m):
@@ -172,6 +180,7 @@
             @pl.when(i == 0)
             def _():
                 c_wait(i)
+                cd_wait(i)
                 load_w(i)
 
             @pl.when(i > 0)
@@ -183,6 +192,7 @@
                     @pl.when(jnp.logical_and(m == 2, i < NA))
                     def _():
                         c_wait(i)
+                        cd_wait(i)
                         load_w(i)
 
                     pre = jnp.dot(u[pl.ds(pl.multiple_of(m * TM, TM), TM), :], w_buf[a % 2],
@@ -212,34 +222,64 @@
         pltpu.VMEM((1, DIM), jnp.float32),
     )
 
-    def phase_b(w_buf, h_buf, x_buf, y_buf):
-        def load_w(j):
-            slot = j % 4
-            for d in others:
+    def phase_b(w_buf, h_buf, x_buf, y_buf, acc_buf):
+        early = [(0, 0, 1), (0, 1, 0), (0, 1, 1), (1, 0, 0), (1, 0, 1)]
+        late = [(1, 1, 0), (1, 1, 1)]
+
+        def load_pieces(j, pieces, sem):
+            slot = j % WS
+            for d in pieces:
                 wf, wx, wk = who(d)
                 r0 = (2 * wx + wk) * F_BLOCK + wf * F_PIECE
                 pltpu.make_async_copy(
                     piece_b(j, (wf, wx, wk)),
                     w_buf.at[slot, pl.ds(pl.multiple_of(r0, 32), F_PIECE), :],
-                    ld_sem.at[slot]).start()
+                    sem.at[slot]).start()
+
+        def load_early(j):
+            c_wait(NA + j)
+            load_pieces(j, early, ld_sem)
             r0 = t * F_BLOCK + f * F_PIECE
             pltpu.make_async_copy(
-                own_b(j), w_buf.at[slot, pl.ds(pl.multiple_of(r0, 32), F_PIECE), :],
-                ld_sem.at[slot]).start()
-
-        def wait_w(j):
+                own_b(j), w_buf.at[j % WS, pl.ds(pl.multiple_of(r0, 32), F_PIECE), :],
+                ld_sem.at[j % WS]).start()
+
+        def load_late(j):
+            cd_wait(NA + j)
+            load_pieces(j, late, ld2_sem)
+
+        def wait_rows(j, n, sem):
             pltpu.make_async_copy(
-                g2.at[:, pl.ds(0, CB)], w_buf.at[j % 4], ld_sem.at[j % 4]).wait()
-
-        def load_h(m, slot):
-            return pltpu.make_async_copy(
-                hbm_h.at[pl.ds(pl.multiple_of(m * TM, TM), TM)], h_buf.at[slot], t_sem.at[slot])
+                g2.at[pl.ds(0, n * F_PIECE), pl.ds(0, CB)],
+                w_buf.at[j % WS, pl.ds(0, n * F_PIECE), :], sem.at[j % WS]).wait()
+
+        def hslot(m):
+            b = (m + MT - RES) // MT
+            return m * (1 - b) + b * (RES + (m + 1) % 2)
+
+        late_cols = [(1 - x) * 2 * F_BLOCK + q * F_BLOCK + (1 - f) * 1664 for q in (0, 1)]
+        ranges = {
+            "all": [(0, FFN)],
+            "early": [(x * 2 * F_BLOCK, 2 * F_BLOCK)] + [
+                ((1 - x) * 2 * F_BLOCK + q * F_BLOCK + f * 1792, 1664) for q in (0, 1)],
+            "late": [(c0, 1792) for c0 in late_cols],
+        }
+
+        def load_h(m, mode):
+            rows = pl.ds(pl.multiple_of(m * TM, TM), TM)
+            if mode != "late":
+                return [pltpu.make_async_copy(
+                    hbm_h.at[rows], h_buf.at[hslot(m)], t_sem.at[(m + 1) % 2, 0])]
+            return [pltpu.make_async_copy(
+                hbm_h.at[rows, pl.ds(pl.multiple_of(c0, 128), 1792)],
+                h_buf.at[hslot(m), :, pl.ds(pl.multiple_of(c0, 128), 1792)],
+                t_sem.at[(m + 1) % 2, q]) for q, c0 in enumerate(late_cols)]
 
         def load_x(m, j, n, slot):
             return pltpu.make_async_copy(
                 hid.at[pl.ds(pl.multiple_of(m * TM, TM), TM),
                        pl.ds(pl.multiple_of(j * CB, 128), n * CB)],
-                x_buf.at[slot, :, pl.ds(0, n * CB)], t_sem.at[2 + slot])
+                x_buf.at[slot, :, pl.ds(0, n * CB)], x_sem.at[slot])
 
         def store_y(m, j, n, slot):
             return pltpu.make_async_copy(
@@ -248,93 +288,141 @@
                        pl.ds(pl.multiple_of(j * CB, 128), n * CB)],
                 o_sem.at[slot, 0])
 
-        def compute(j, n, hooks):
+        def compute(j, n, mode, hooks):
+            last = mode != "early"
             for q in range(n):
-                wait_w(j + q)
-            load_h(0, 0).start()
-            load_x(0, j, n, 0).start()
+                if mode != "late":
+                    wait_rows(j + q, 6, ld_sem)
+                if last:
+                    wait_rows(j + q, 2, ld2_sem)
+            if last:
+                load_x(0, j, n, 0).start()
 
             @pl.loop(0, MT)
             def _(m):
                 slot = m % 2
 
-                @pl.when(m + 1 < MT)
+                @pl.when(m == 0)
                 def _():
-                    load_h(m + 1, 1 - slot).start()
-                    load_x(m + 1, j, n, 1 - slot).start()
-
+                    for mm in (RES, RES + 1):
+                        for c in load_h(mm, mode):
+                            c.start()
+
+                if last:
+                    pl.when(m + 1 < MT)(lambda: load_x(m + 1, j, n, 1 - slot).start())
                 for at, hook in hooks.items():
                     pl.when(m == at)(hook)
-                load_h(m, slot).wait()
-                load_x(m, j, n, slot).wait()
-
-                @pl.when(m >= 2)
+
+                @pl.when(m >= RES)
                 def _():
-                    store_y(m, j, n, slot).wait()
-
+                    for c in load_h(m, mode):
+                        c.wait()
+
+                if last:
+                    load_x(m, j, n, slot).wait()
+
+                    @pl.when(m >= 2)
+                    def _():
+                        store_y(m, j, n, slot).wait()
+
+                rows = pl.ds(pl.multiple_of(m * TM, TM), TM)
                 for q in range(n):
-                    cols = slice(q * CB, (q + 1) * CB)
-                    acc = jnp.dot(h_buf[slot], w_buf[(j + q) % 4],
-                                  preferred_element_type=jnp.float32)
-                    y_buf[slot, :, cols] = (
-                        x_buf[slot, :, cols].astype(jnp.float32) + acc).astype(jnp.bfloat16)
-                store_y(m, j, n, slot).start()
-
-            for m in (MT - 2, MT - 1):
-                store_y(m, j, n, m % 2).wait()
-
+                    acc = None
+                    for c0, size in ranges[mode]:
+                        kk = slice(None) if mode == "all" else pl.ds(pl.multiple_of(c0, 128), size)
+                        part = jnp.dot(h_buf[hslot(m), :, kk], w_buf[(j + q) % WS, kk, :],
+                                       preferred_element_type=jnp.float32)
+                        acc = part if acc is None else acc + part
+                    if mode == "early":
+                        acc_buf[j - (NB - 2), rows, :] = acc
+                    else:
+                        if mode == "late":
+                            acc = acc + acc_buf[j + q - (NB - 2), rows, :]
+                        cols = slice(q * CB, (q + 1) * CB)
+                        y_buf[slot, :, cols] = (
+                            x_buf[slot, :, cols].astype(jnp.float32) + acc).astype(jnp.bfloat16)
+                if last:
+                    store_y(m, j, n, slot).start()
+
+                @pl.when(jnp.logical_and(m >= RES, m + 2 < MT))
+                def _():
+                    for c in load_h(m + 2, mode):
+                        c.start()
+
+            if last:
+                for m in (MT - 2, MT - 1):
+                    store_y(m, j, n, m % 2).wait()
+
+        for m in range(RES):
+            pltpu.make_async_copy(
+                hbm_h.at[pl.ds(m * TM, TM)], h_buf.at[m], t_sem.at[m % 2, m // 2]).start()
         d_point(NA)
+        load_early(0)
+        load_late(0)
         comm_point(NA + 2)
         d_point(NA + 1)
-        for n in (0, 1):
-            c_wait(NA + n)
-            load_w(n)
-
-        @pl.loop(1, NPAIR + 1)
+        for m in range(RES):
+            pltpu.make_async_copy(
+                hbm_h.at[pl.ds(m * TM, TM)], h_buf.at[m], t_sem.at[m % 2, m // 2]).wait()
+
+        def pair(j):
+            load_early(j + 1)
+            load_late(j + 1)
+
+            def load():
+                load_early(j + 2)
+                load_late(j + 2)
+
+            compute(j, 2, "all", {
+                3: lambda: comm_point(NA + j + 3),
+                6: lambda: d_point(NA + j + 2),
+                7: load,
+            })
+
+        n_pairs = (NB - 4) // 2
+
+        @pl.loop(0, n_pairs)
         def _(p):
-            j = 2 * p
-            comm_point(NA + j + 1)
-            d_point(NA + j)
-
-            def mid():
-                comm_point(NA + j + 2)
-                d_point(NA + j + 1)
-
-            def load():
-                for q in (0, 1):
-                    c_wait(NA + j + q)
-                    load_w(j + q)
-
-            compute(j - 2, 2, {3: mid, 5: load})
-
-        j = 2 * NPAIR
-
-        def next_comm():
-            comm_point(NA + j + 3)
-            d_point(NA + j + 2)
-
-        def next_load():
-            c_wait(NA + j + 2)
-            load_w(j + 2)
-
-        def last_d():
-            d_point(NA + j + 3)
+            pair(2 * p)
+
+            @pl.when(p < n_pairs - 1)
+            def _():
+                comm_point(NA + 2 * p + 4)
+                d_point(NA + 2 * p + 3)
+
+        j = NB - 4
+        compute(j, 1, "all", {
+            0: lambda: load_early(j + 1),
+            3: lambda: comm_point(NA + j + 2),
+            7: lambda: d_point(NA + j + 1),
+        })
+        load_late(j + 1)
+        compute(j + 1, 1, "all", {
+            1: lambda: load_early(j + 2),
+            7: lambda: comm_point(NA + j + 3),
+        })
+        compute(j + 2, 1, "early", {
+            2: lambda: load_early(j + 3),
+            7: lambda: d_point(NA + j + 2),
+        })
 
         def last_load():
-            c_wait(NA + j + 3)
-            load_w(j + 3)
-
-        compute(j, 1, {})
-        compute(j + 1, 1, {0: next_comm, 2: next_load})
-        compute(j + 2, 1, {2: last_d, 3: last_load})
-        compute(j + 3, 1, {})
+            load_late(j + 3)
+
+        compute(j + 3, 1, "early", {
+            1: lambda: load_late(j + 2),
+            5: lambda: d_point(NA + j + 3),
+            7: last_load,
+        })
+        compute(j + 2, 2, "late", {})
 
     pl.run_scoped(
         phase_b,
-        pltpu.VMEM((4, FFN, CB), jnp.bfloat16),
-        pltpu.VMEM((2, TM, FFN), jnp.bfloat16),
+        pltpu.VMEM((WS, FFN, CB), jnp.bfloat16),
+        pltpu.VMEM((RES + 2, TM, FFN), jnp.bfloat16),
         pltpu.VMEM((2, TM, 2 * CB), jnp.bfloat16),
         pltpu.VMEM((2, TM, 2 * CB), jnp.bfloat16),
+        pltpu.VMEM((2, ROWS, CB), jnp.float32),
     )
 
     for kind in range(9):
@@ -365,13 +453,16 @@
                 pltpu.SemaphoreType.DMA((S,)),
                 pltpu.SemaphoreType.DMA((S,)),
                 pltpu.SemaphoreType.DMA((S,)),
+                pltpu.SemaphoreType.DMA((S,)),
                 pltpu.SemaphoreType.DMA((2, 9)),
-                pltpu.SemaphoreType.DMA((4,)),
-                pltpu.SemaphoreType.DMA((4,)),
+                pltpu.SemaphoreType.DMA((WS,)),
+                pltpu.SemaphoreType.DMA((WS,)),
+                pltpu.SemaphoreType.DMA((2, 2)),
+                pltpu.SemaphoreType.DMA((2,)),
                 pltpu.SemaphoreType.DMA((2, 4)),
             ],
             compiler_params=pltpu.CompilerParams(
-                collective_id=0, has_side_effects=True, vmem_limit_bytes=60 * 2**20),
+                collective_id=0, has_side_effects=True, vmem_limit_bytes=63 * 2**20),
             name="mlp",
         )(hidden, ln_scale.reshape(1, DIM), w_in, w_out)
         return y

time: 1250 us -> 1210 us (0.968)
  Pallas kernels: 1230 us -> 1190 us
    pallas_call x1, Pallas kernels: 1230 us -> 1190 us  [local_mlp(): pl.pallas_call(kernel, out_shape=[jax.ShapeDtypeStruct((ROWS, DIM), bf16)...]
where the time goes in v2:
time: 1210 us
  Pallas kernels  1190 us (98%)
  local copies, waits for them, and re-layouts  17.3 us (1%)
    pallas_call x1, Pallas kernels, local_mlp(): pl.pallas_call(kernel, out_shape=[jax.ShapeDtypeStruct((ROWS, DIM), bf16)...  1190 us

profile of v2, /device:TPU:0, one launch (start us, length us, event | category | flops | bytes accessed | tf_op | source)
XLA Modules:
  0.0 1207.6 jit_solution(12485517212158730843)
XLA Ops:
  0.0 1190.3 %mlp.1 = (bf16[2048,5120]{1,0:T(8,128)(2,1)}, bf16[27,5120,512]{2,1,0:T(8,128)(2,1)}, bf16[13824,5120]{1,0:T(8,128)(2,1)}, bf16[2048,13824]{1,0:T(8,128)(2,1)}) custom-call(bf16[2048,5120]{1,0:T(8,128)(2,1)} %hid.1, f32[1,5120]{1,0:T(1,128)} %bitcast.1, bf16[2560,3456]{1,0:T(8,128)(2,1)} %w_in.1, bf16[1728,5120]{1,0:T(8,128)(2,1)} %w_out.1), custom_call_target="tpu_custom_call" | custom-call | tf_op jit(solution)/shard_map/mlp/pallas_call | solution.py:440
  1190.3 17.3 %copy.6 = bf16[2048,5120]{1,0:T(8,128)(2,1)} copy(bf16[2048,5120]{1,0:T(8,128)(2,1)} %get-tuple-element.6) | data formatting | bytes 41943040

commit v3 on v2

--- a/solution.py
+++ b/solution.py
@@ -17,8 +17,9 @@
 LEAD = 2
 TM = 256
 MT = ROWS // TM
+KS = 1152
 WS = 3
-RES = 1
+RES = 3
 
 
 def kernel(hid, gain, w_in, w_out, out, g1, g2, hbm_h,
@@ -259,8 +260,8 @@
 
         late_cols = [(1 - x) * 2 * F_BLOCK + q * F_BLOCK + (1 - f) * 1664 for q in (0, 1)]
         ranges = {
-            "all": [(0, FFN)],
-            "early": [(x * 2 * F_BLOCK, 2 * F_BLOCK)] + [
+            "all": [(q * KS, KS) for q in range(FFN // KS)],
+            "early": [(x * 2 * F_BLOCK + q * KS, KS) for q in range(2 * F_BLOCK // KS)] + [
                 ((1 - x) * 2 * F_BLOCK + q * F_BLOCK + f * 1792, 1664) for q in (0, 1)],
             "late": [(c0, 1792) for c0 in late_cols],
         }
@@ -329,7 +330,7 @@
                 for q in range(n):
                     acc = None
                     for c0, size in ranges[mode]:
-                        kk = slice(None) if mode == "all" else pl.ds(pl.multiple_of(c0, 128), size)
+                        kk = slice(c0, c0 + size) if mode == "all" else pl.ds(pl.multiple_of(c0, 128), size)
                         part = jnp.dot(h_buf[hslot(m), :, kk], w_buf[(j + q) % WS, kk, :],
                                        preferred_element_type=jnp.float32)
                         acc = part if acc is None else acc + part

time: 1210 us -> 1200 us (level)
  no operation moved by 1% of the time
where the time goes in v3:
time: 1200 us
  Pallas kernels  1190 us (99%)
  local copies, waits for them, and re-layouts  17.3 us (1%)
    pallas_call x1, Pallas kernels, local_mlp(): pl.pallas_call(kernel, out_shape=[jax.ShapeDtypeStruct((ROWS, DIM), bf16)...  1190 us

profile of v3, /device:TPU:0, one launch (start us, length us, event | category | flops | bytes accessed | tf_op | source)
XLA Modules:
  0.0 1203.4 jit_solution(1086146689181170779)
XLA Ops:
  0.0 1186.1 %mlp.1 = (bf16[2048,5120]{1,0:T(8,128)(2,1)}, bf16[27,5120,512]{2,1,0:T(8,128)(2,1)}, bf16[13824,5120]{1,0:T(8,128)(2,1)}, bf16[2048,13824]{1,0:T(8,128)(2,1)}) custom-call(bf16[2048,5120]{1,0:T(8,128)(2,1)} %hid.1, f32[1,5120]{1,0:T(1,128)} %bitcast.1, bf16[2560,3456]{1,0:T(8,128)(2,1)} %w_in.1, bf16[1728,5120]{1,0:T(8,128)(2,1)} %w_out.1), custom_call_target="tpu_custom_call" | custom-call | tf_op jit(solution)/shard_map/mlp/pallas_call | solution.py:441
  1186.1 17.3 %copy.6 = bf16[2048,5120]{1,0:T(8,128)(2,1)} copy(bf16[2048,5120]{1,0:T(8,128)(2,1)} %get-tuple-element.6) | data formatting | bytes 41943040
